TPU v7x, 32 devices: a whole 2x2x4 slice. The times are simulated.
32 devices in a mesh: ctx: 32 (over z, y, x, core).
Axes of the slice: x: 2, y: 2, z: 4, core: 2. Of those that a mesh axis runs over, the one named last changes fastest.
Arguments:
- queries: bfloat16 [8192, 768], P('ctx'), may hold values from -16 to 16
- keys: bfloat16 [8192, 768], P('ctx'), may hold values from -16 to 16
- values: bfloat16 [8192, 768], P('ctx'), may hold values from -6 to 6
- offsets: int32 [5, 12], replicated, may hold values from 0 to 31, as said below
Outputs:
- attended: bfloat16 [8192, 768], P('ctx')
Inputs may be any that keep to these rules, and one draw needn't show every extreme that they name: offsets[l, h] lies in 0 to min(4 ** l, 32) - 1.
All inputs are finite; a program needn't handle non-finite values.
Results may differ from a plain program's by a relative error of at most 0.0035.
Values may be sent and summed in bfloat16 or wider, within the bound.
A program may use at most 64 MiB of HBM per device.

v0:
```python
import functools

import jax
import jax.numpy as jnp
from jax import lax
from jax.experimental import pallas as pl
from jax.experimental.pallas import tpu as pltpu
from jax.sharding import PartitionSpec as P

MESH = pl.DeviceIdType.MESH


def plan_of(levels, count, tokens, heads):
    plan = []
    late = False
    for height in range(1, levels):
        group = min(4**height, count)
        per = -(-heads // group)
        shift = 0
        if group >= 2 * heads:
            shift = group // 4 + (group // 2 - heads if late else 0)
            late = not late
        plan.append((height, group, tokens // group, per, shift))
    return plan


def is_packed(rows):
    return rows % 32 == 0


def halves(shape):
    return lax.broadcasted_iota(jnp.int32, shape, 1) < shape[1] // 2


def swap_halves(value):
    return pltpu.roll(value.astype(jnp.float32), value.shape[1] // 2, 1)


def causal_unit(query, key, value):
    tokens = query.shape[0]
    half = tokens // 2
    outs, peaks = [], []
    for start in (0, half):
        end = start + half
        scores = lax.dot_general(
            query[start:end],
            key[:end],
            (((1,), (1,)), ((), ())),
            preferred_element_type=jnp.float32,
        )
        rows = lax.broadcasted_iota(jnp.int32, scores.shape, 0) + start
        cols = lax.broadcasted_iota(jnp.int32, scores.shape, 1)
        scores = jnp.where(cols <= rows, scores, -1e30)
        peak = jnp.max(scores, axis=1, keepdims=True)
        weights = jnp.exp(scores - peak).astype(jnp.bfloat16)
        outs.append(jnp.dot(weights, value[:end], preferred_element_type=jnp.float32))
        peaks.append(peak)
    return jnp.concatenate(outs, 0), jnp.concatenate(peaks, 0)


def exchange_kernel(plan, heads, scale, offs, q_ref, k_ref, v_ref, out_ref, *scratch):
    number = len(plan)
    stage = scratch[:number]
    inbox = scratch[number : 2 * number]
    outbox = scratch[2 * number : 3 * number]
    back = scratch[3 * number : 4 * number]
    numer, total, peaks, send_sem, recv_sem, ret_send, ret_recv = scratch[4 * number :]
    tokens = q_ref.shape[0]
    pair = 2 * (q_ref.shape[1] // heads)
    pairs = heads // 2
    me = lax.axis_index("ctx")
    count = lax.axis_size("ctx")

    barrier = pltpu.get_barrier_semaphore()

    def owns(device, entry):
        _, group, _, per, shift = entry
        return lax.rem(lax.rem(device, group) + group - shift, group) * per < heads

    def greet(step, carry):
        other = lax.rem(me + step, count)
        meets = False
        for entry in plan:
            group = entry[1]
            same = lax.div(me, group) == lax.div(other, group)
            meets = jnp.logical_or(
                meets, jnp.logical_and(same, jnp.logical_or(owns(me, entry), owns(other, entry)))
            )

        @pl.when(meets)
        def _():
            pl.semaphore_signal(barrier, inc=1, device_id=(other,), device_id_type=MESH)

        return carry + jnp.where(meets, 1, 0)

    partners = lax.fori_loop(1, count, greet, 0)

    picked = sum(rows for _, _, rows, _, _ in plan)
    row_id = lax.broadcasted_iota(jnp.int32, (picked, tokens), 0)
    col_id = lax.broadcasted_iota(jnp.int32, (picked, tokens), 1)
    low_p = halves((picked, pair))

    def pick(p, carry):
        cols = pl.ds(pl.multiple_of(p * pair, pair), pair)
        packed = jnp.concatenate([q_ref[:, cols], k_ref[:, cols], v_ref[:, cols]], 1)
        for side in range(2):
            head = 2 * p + side
            first = 0
            target = jnp.zeros((picked, tokens), jnp.int32)
            for height, group, rows, _, _ in plan:
                here = (row_id - first) * group + offs[height, head]
                target = here if first == 0 else jnp.where(row_id < first, target, here)
                first += rows
            hit = jnp.where(col_id == target, 1.0, 0.0).astype(jnp.bfloat16)
            got = jnp.dot(hit, packed, preferred_element_type=jnp.float32)
            query, key, value = got[:, :pair], got[:, pair : 2 * pair], got[:, 2 * pair :]
            swapped = swap_halves(value)
            if side == 0:
                key = swap_halves(key)
            else:
                query = swap_halves(query)
                value, swapped = swapped, value
            left = jnp.where(low_p, query * scale, key)
            first = 0
            for at, (_, _, rows, _, _) in enumerate(plan):
                kind = stage[at].dtype
                last = first + rows
                if is_packed(rows):
                    middle = first + rows // 2
                    right = jnp.where(
                        low_p[: rows // 2], value[first:middle], swapped[middle:last]
                    )
                    stage[at][head] = jnp.concatenate([left[first:last], right], 0).astype(kind)
                else:
                    stage[at][head] = jnp.concatenate(
                        [left[first:last], value[first:last]], 1
                    ).astype(kind)
                first = last
        return carry

    lax.fori_loop(0, pairs, pick, 0)
    pl.semaphore_wait(barrier, partners)

    def place(entry, head):
        _, group, _, per, shift = entry
        where = lax.rem(shift + head // per, group)
        mine = lax.rem(me, group)
        return me - mine + where, where == mine, mine, head % per

    def sending(at, head):
        owner, _, mine, slot = place(plan[at], head)
        return pltpu.make_async_remote_copy(
            src_ref=stage[at].at[head],
            dst_ref=inbox[at].at[slot, mine],
            send_sem=send_sem.at[at, head],
            recv_sem=recv_sem.at[at, slot],
            device_id=(owner,),
            device_id_type=MESH,
        )

    order = list(range(number))[::-1]
    for at in order:

        def push(head, carry, at=at):
            _, own, mine, slot = place(plan[at], head)

            @pl.when(jnp.logical_not(own))
            def _():
                sending(at, head).start()

            @pl.when(own)
            def _():
                inbox[at][slot, mine] = stage[at][head]

            return carry

        lax.fori_loop(0, heads, push, 0)

    low = halves((tokens, pair))

    def base(p, carry):
        cols = pl.ds(pl.multiple_of(p * pair, pair), pair)
        query = q_ref[:, cols].astype(jnp.float32) * scale
        key = k_ref[:, cols]
        value = v_ref[:, cols].astype(jnp.float32)
        got = []
        for side in range(2):
            mask = low if side == 0 else jnp.logical_not(low)
            got.append(
                causal_unit(
                    jnp.where(mask, query, 0.0).astype(jnp.bfloat16),
                    key,
                    jnp.where(mask, value, 1.0).astype(jnp.bfloat16),
                )
            )
        numer[:, cols] = jnp.where(low, got[0][0], got[1][0])
        total[:, cols] = swap_halves(jnp.where(low, got[1][0], got[0][0]))
        peaks[:, cols] = jnp.where(low, got[0][1], got[1][1])
        return carry

    lax.fori_loop(0, 2 * pairs // 3, base, 0)

    lane = lax.broadcasted_iota(jnp.int32, (tokens, pair), 1)
    mid_lane = pair // 2

    def returning(at, slot, head, there):
        _, group, _, _, _ = plan[at]
        mine = lax.rem(me, group)
        return pltpu.make_async_remote_copy(
            src_ref=outbox[at].at[slot, there],
            dst_ref=back[at].at[head],
            send_sem=ret_send.at[at, slot],
            recv_sem=ret_recv.at[at, head],
            device_id=(me - mine + there,),
            device_id_type=MESH,
        )

    def owned(at, slot):
        _, group, _, per, shift = plan[at]
        mine = lax.rem(me, group)
        head = lax.rem(mine + group - shift, group) * per + slot
        return head, mine

    for at in order:
        _, group, rows, per, _ = plan[at]
        for slot in range(per):
            head, mine = owned(at, slot)

            @pl.when(head < heads)
            def _(at=at, group=group, rows=rows, slot=slot, head=head, mine=mine):
                arrived = inbox[at].at[slot, pl.ds(0, group - 1)]
                pltpu.make_async_copy(arrived, arrived, recv_sem.at[at, slot]).wait()
                block = inbox[at][slot]
                if is_packed(rows):
                    left = block[:, :rows].reshape(tokens, pair).astype(jnp.float32)
                    right = block[:, rows:].reshape(tokens // 2, pair).astype(jnp.float32)
                    split = (group, rows // 2, pair)
                    right = jnp.concatenate(
                        [right.reshape(split), swap_halves(right).reshape(split)], 1
                    ).reshape(tokens, pair)
                else:
                    block = block.reshape(tokens, 2 * pair)
                    left = block[:, :pair].astype(jnp.float32)
                    right = block[:, pair:].astype(jnp.float32)
                value = jnp.where(low, right, 1.0).astype(jnp.bfloat16)
                query = jnp.where(low, left, 0.0).astype(jnp.bfloat16)
                key = swap_halves(left).astype(jnp.bfloat16)
                got, peak = causal_unit(query, key, value)
                lse = peak + jnp.log(jnp.where(low, 1.0, got))
                hi = lse.astype(jnp.bfloat16).astype(jnp.float32)
                rest = lse - hi
                mid = rest.astype(jnp.bfloat16).astype(jnp.float32)
                parts = jnp.where(lane == mid_lane, hi, 0.0)
                parts = jnp.where(lane == mid_lane + 1, mid, parts)
                parts = jnp.where(lane == mid_lane + 2, rest - mid, parts)
                result = jnp.where(low, got / jnp.where(low, swap_halves(got), 1.0), parts)
                outbox[at][slot] = result.reshape(group, rows, pair).astype(outbox[at].dtype)

                def give(step, carry):
                    returning(at, slot, head, lax.rem(mine + step, group)).start()
                    return carry

                lax.fori_loop(1, group, give, 0)
                back[at][head] = outbox[at][slot, mine]

    lax.fori_loop(2 * pairs // 3, pairs, base, 0)

    def collect(at):
        def one(head, carry):
            _, own, mine, slot = place(plan[at], head)

            @pl.when(jnp.logical_not(own))
            def _():
                sending(at, head).wait_send()
                returning(at, slot, head, mine).wait_recv()

            return carry

        lax.fori_loop(0, heads, one, 0)

    for at in order:
        collect(at)

    token = lax.broadcasted_iota(jnp.int32, (tokens, 1), 0)

    def merge(p, carry):
        cols = pl.ds(pl.multiple_of(p * pair, pair), pair)
        values, lses = [], []
        for at, (height, group, rows, _, _) in enumerate(plan):
            spread = lax.broadcasted_iota(jnp.int32, (tokens, rows), 0)
            source = lax.broadcasted_iota(jnp.int32, (tokens, rows), 1)
            got, lse = [], []
            for side in range(2):
                head = 2 * p + side
                offset = offs[height, head]
                hit = jnp.where(spread == source * group + offset, 1.0, 0.0).astype(jnp.bfloat16)
                sent = back[at][head]
                if side == 1:
                    sent = swap_halves(sent)
                moved = jnp.dot(hit, sent.astype(jnp.bfloat16), preferred_element_type=jnp.float32)
                other = jnp.logical_not(low) if side == 0 else low
                level_lse = jnp.sum(jnp.where(other, moved, 0.0), axis=1, keepdims=True)
                kept = jnp.bitwise_and(token, group - 1) == offset
                lse.append(jnp.where(kept, level_lse, -1e30))
                got.append(moved)
            values.append(jnp.where(low, got[0], got[1]))
            lses.append(jnp.where(low, lse[0], lse[1]))
        best = peaks[:, cols]
        for lse in lses:
            best = jnp.maximum(best, lse)
        keep = jnp.exp(peaks[:, cols] - best)
        top = numer[:, cols] * keep
        bottom = total[:, cols] * keep
        for value, lse in zip(values, lses):
            share = jnp.exp(lse - best)
            top = top + value * share
            bottom = bottom + share
        out_ref[:, cols] = (top / bottom).astype(out_ref.dtype)
        return carry

    lax.fori_loop(0, pairs, merge, 0, unroll=2)

    for at in order:
        _, group, _, per, _ = plan[at]
        for slot in range(per):
            head, _ = owned(at, slot)

            @pl.when(head < heads)
            def _(at=at, group=group, slot=slot):
                gone = outbox[at].at[slot, pl.ds(0, group - 1)]
                pltpu.make_async_copy(gone, gone, ret_send.at[at, slot]).wait()


def exchange_body(queries, keys, values, offsets):
    tokens, model = queries.shape
    levels, heads = offsets.shape
    count = lax.axis_size("ctx")
    plan = plan_of(levels, count, tokens, heads)
    pair = 2 * (model // heads)
    number = len(plan)
    most = max(entry[3] for entry in plan)

    def dtype(rows):
        return jnp.bfloat16 if rows % 8 == 0 else jnp.float32

    def block(rows):
        return (rows + rows // 2, pair) if is_packed(rows) else (rows, 2 * pair)

    scratch = []
    for _, group, rows, per, _ in plan:
        scratch.append(pltpu.VMEM((heads, *block(rows)), dtype(rows)))
    for _, group, rows, per, _ in plan:
        scratch.append(pltpu.VMEM((per, group, *block(rows)), dtype(rows)))
    for _, group, rows, per, _ in plan:
        scratch.append(pltpu.VMEM((per, group, rows, pair), dtype(rows)))
    for _, group, rows, per, _ in plan:
        scratch.append(pltpu.VMEM((heads, rows, pair), dtype(rows)))
    scratch += [pltpu.VMEM((tokens, model), jnp.float32)] * 3
    scratch += [
        pltpu.SemaphoreType.DMA((number, heads)),
        pltpu.SemaphoreType.DMA((number, most)),
        pltpu.SemaphoreType.DMA((number, most)),
        pltpu.SemaphoreType.DMA((number, heads)),
    ]
    scale = (model // heads) ** -0.5
    vmem = pl.BlockSpec(memory_space=pltpu.VMEM)
    return pl.pallas_call(
        functools.partial(exchange_kernel, plan, heads, scale),
        out_shape=jax.ShapeDtypeStruct((tokens, model), jnp.bfloat16),
        in_specs=[pl.BlockSpec(memory_space=pltpu.SMEM), vmem, vmem, vmem],
        out_specs=vmem,
        scratch_shapes=scratch,
        compiler_params=pltpu.CompilerParams(collective_id=0, has_side_effects=True),
    )(offsets, queries, keys, values)


def solution(mesh):
    in_specs = (P("ctx", None), P("ctx", None), P("ctx", None), P())
    out_specs = P("ctx", None)
    return jax.shard_map(
        exchange_body, mesh=mesh, in_specs=in_specs, out_specs=out_specs, check_vma=False
    )
```

profile of v0, /device:TPU:17, one launch (start us, length us, event | category | flops | bytes accessed | tf_op | source)
XLA Modules:
  0.0 27.1 jit_solution(8210419379161999999)
XLA Ops:
  0.0 25.3 %shard_map.46 = bf16[256,768]{1,0:T(8,128)(2,1)} custom-call(s32[5,12]{1,0:T(8,128)} %offs.1, bf16[256,768]{1,0:T(8,128)(2,1)} %q_ref.1, bf16[256,768]{1,0:T(8,128)(2,1)} %k_ref.1, bf16[256,768]{1,0:T(8,128)(2,1)} %v_ref.1), custom_call_target="tpu_custom_call" | custom-call | tf_op jit(solution)/shard_map/pallas_call | solution.py:367
  25.3 1.8 %copy.6 = bf16[256,768]{1,0:T(8,128)(2,1)} copy(bf16[256,768]{1,0:T(8,128)(2,1)} %shard_map.46) | data formatting | bytes 786432
where the time goes:
time: 27.2 us; the launch traced here: 27.1 us
  Pallas kernels  25.3 us (93%)
  local copies, waits for them, and re-layouts  1.77 us (7%)
    pallas_call x1, Pallas kernels, exchange_body(): pl.pallas_call(functools.partial(exchange_kernel, plan, heads, scale), ou...  25.3 us
    unnamed x1, local copies, waits for them, and re-layouts  1.77 us

commit v1 on v0

v1 whole, which is shorter than its diff:
```python
import functools

import jax
import jax.numpy as jnp
from jax import lax
from jax.experimental import pallas as pl
from jax.experimental.pallas import tpu as pltpu
from jax.sharding import PartitionSpec as P

MESH = pl.DeviceIdType.MESH
NEG = -1e30
LAST = (((1,), (1,)), ((), ()))


def plan_of(levels, count, tokens, heads):
    plan = []
    late = False
    for height in range(1, levels):
        group = min(4**height, count)
        per = -(-heads // group)
        shift = 0
        if group >= 2 * heads:
            shift = group // 4 + (group // 2 - heads if late else 0)
            late = not late
        plan.append((height, group, tokens // group, per, shift))
    return plan


def is_packed(rows):
    return rows % 32 == 0


def up8(rows):
    return -(-rows // 8) * 8


def kind_of(rows):
    return jnp.bfloat16 if rows % 8 == 0 else jnp.float32


def halves(shape):
    return lax.broadcasted_iota(jnp.int32, shape, 1) < shape[1] // 2


def swap_halves(value):
    return pltpu.roll(value.astype(jnp.float32), value.shape[1] // 2, 1)


def attend(keys, queries, values_t):
    half = keys.shape[0] // 2
    scores = lax.dot_general(keys[:half], queries, LAST, preferred_element_type=jnp.float32)
    corner = lax.dot_general(
        keys[half:], queries[half:], LAST, preferred_element_type=jnp.float32
    )
    rows = lax.broadcasted_iota(jnp.int32, (half, half), 0)
    cols = lax.broadcasted_iota(jnp.int32, (half, half), 1)
    allowed = rows <= cols
    left = jnp.where(allowed, scores[:, :half], NEG)
    upper = scores[:, half:]
    lower = jnp.where(allowed, corner, NEG)
    peak_l = jnp.max(left, axis=0, keepdims=True)
    peak_r = jnp.maximum(
        jnp.max(upper, axis=0, keepdims=True), jnp.max(lower, axis=0, keepdims=True)
    )
    left = jnp.exp(left - peak_l).astype(jnp.bfloat16)
    upper = jnp.exp(upper - peak_r).astype(jnp.bfloat16)
    lower = jnp.exp(lower - peak_r).astype(jnp.bfloat16)
    out_l = jnp.dot(values_t[:, :half], left, preferred_element_type=jnp.float32)
    out_r = jnp.dot(
        values_t, jnp.concatenate([upper, lower], 0), preferred_element_type=jnp.float32
    )
    return jnp.concatenate([out_l, out_r], 1), jnp.concatenate([peak_l, peak_r], 1)


def places(plan, tokens):
    parts = []
    for _, group, rows, _, _ in plan:
        shape = (up8(rows), tokens)
        row = lax.broadcasted_iota(jnp.int32, shape, 0)
        col = lax.broadcasted_iota(jnp.int32, shape, 1)
        part = col - row * group
        parts.append(part if rows % 8 == 0 else jnp.where(row < rows, part, -1))
    return parts


def exchange_kernel(plan, heads, scale, offs_hbm, q_hbm, k_hbm, v_hbm, *refs):
    number = len(plan)
    base_out, base_peak, base_total, hits_out = refs[:4]
    back = refs[4 : 4 + number]
    refs = refs[4 + number :]
    offs, q_ref, k_ref, v_ref = refs[:4]
    refs = refs[4:]
    stage = refs[:number]
    inbox = refs[number : 2 * number]
    outbox = refs[2 * number : 3 * number]
    in_sem, send_sem, recv_sem, ret_send, ret_recv = refs[3 * number :]
    tokens, model = q_ref.shape
    size = model // heads
    pair = 2 * size
    pairs = heads // 2
    me = lax.axis_index("ctx")
    count = lax.axis_size("ctx")

    moves = [(offs_hbm, offs), (q_hbm, q_ref), (k_hbm, k_ref), (v_hbm, v_ref)]
    loads = [
        pltpu.make_async_copy(source, target, in_sem.at[i])
        for i, (source, target) in enumerate(moves)
    ]
    for load in loads:
        load.start()

    barrier = pltpu.get_barrier_semaphore()

    def greet(step, carry):
        other = lax.rem(me + step, count)
        pl.semaphore_signal(barrier, inc=1, device_id=(other,), device_id_type=MESH)
        return carry

    with jax.named_scope("greet"):
        lax.fori_loop(1, count, greet, 0)

    low = halves((tokens, pair))
    spans = [up8(entry[2]) for entry in plan]
    starts = [sum(spans[:at]) for at in range(number)]
    picked = sum(spans)
    low_p = halves((picked, pair))
    where_p = places(plan, tokens)

    with jax.named_scope("loadw"):
        for load in loads:
            load.wait()

    def pick(p, carry):
        cols = pl.ds(pl.multiple_of(p * pair, pair), pair)
        packed = jnp.concatenate([q_ref[:, cols], k_ref[:, cols], v_ref[:, cols]], 1)
        hits = []
        for side in range(2):
            for at, (height, *_) in enumerate(plan):
                hits.append(jnp.where(where_p[at] == offs[height, 2 * p + side], 1.0, 0.0))
        hit = jnp.concatenate(hits, 0).astype(jnp.bfloat16)
        hits_out[p] = hit
        both = jnp.dot(hit, packed, preferred_element_type=jnp.float32)
        for side in range(2):
            head = 2 * p + side
            got = both[side * picked : (side + 1) * picked]
            query, key, value = got[:, :pair], got[:, pair : 2 * pair], got[:, 2 * pair :]
            swapped = swap_halves(value)
            if side == 0:
                key = swap_halves(key)
            else:
                query = swap_halves(query)
                value, swapped = swapped, value
            left = jnp.where(low_p, query * scale, key)
            for at, (_, _, rows, _, _) in enumerate(plan):
                kind = stage[at].dtype
                first = starts[at]
                last = first + rows
                if is_packed(rows):
                    middle = first + rows // 2
                    right = jnp.where(
                        low_p[: rows // 2], value[first:middle], swapped[middle:last]
                    )
                    stage[at][head] = jnp.concatenate([left[first:last], right], 0).astype(kind)
                else:
                    stage[at][head] = jnp.concatenate(
                        [left[first:last], value[first:last]], 1
                    ).astype(kind)
        return carry

    with jax.named_scope("pick"):
        lax.fori_loop(0, pairs, pick, 0, unroll=3)
    with jax.named_scope("barw"):
        pl.semaphore_wait(barrier, count - 1)

    seats, seat = [], 0
    for _, _, _, per, _ in plan:
        seats.append(seat)
        seat += per

    def spot(at):
        _, group, _, _, shift = plan[at]
        mine = lax.rem(me, group)
        return mine, lax.rem(mine + group - shift, group)

    order = list(range(number))[::-1]
    with jax.named_scope("push"):
        for at in order:
            _, group, _, per, shift = plan[at]
            mine, _ = spot(at)
            for head in sorted(range(heads), key=lambda h: h % per):
                where = (shift + head // per) % group
                slot = head % per
                target = inbox[at].at[slot, mine]
                arrived = recv_sem.at[seats[at] + slot]

                @pl.when(mine != where)
                def _(at=at, head=head, where=where, target=target, arrived=arrived, mine=mine):
                    pltpu.make_async_remote_copy(
                        src_ref=stage[at].at[head],
                        dst_ref=target,
                        send_sem=send_sem.at[at],
                        recv_sem=arrived,
                        device_id=(me - mine + where,),
                        device_id_type=MESH,
                    ).start()

                @pl.when(mine == where)
                def _(at=at, head=head, target=target, arrived=arrived):
                    pltpu.make_async_copy(stage[at].at[head], target, arrived).start()

    ones = jnp.ones((16, tokens), jnp.bfloat16)
    row8 = lax.broadcasted_iota(jnp.int32, (8, tokens), 0)

    def base(p, carry):
        cols = pl.ds(pl.multiple_of(p * pair, pair), pair)
        query = q_ref[:, cols].astype(jnp.float32) * scale
        key = k_ref[:, cols]
        value_t = v_ref[:, cols].T
        for side in range(2):
            mask = low if side == 0 else jnp.logical_not(low)
            got, peak = attend(
                key,
                jnp.where(mask, query, 0.0).astype(jnp.bfloat16),
                jnp.concatenate([value_t[side * size : (side + 1) * size], ones], 0),
            )
            head = 2 * p + side
            base_out[head] = got[:size]
            base_peak[head] = jnp.where(row8 == number, peak, NEG)
            base_total[head] = jnp.where(row8 == number, got[size : size + 1], 1.0)
        return carry

    cuts = [pairs * part // 3 for part in range(4)]

    def bases(part):
        with jax.named_scope(f"base{part}"):
            lax.fori_loop(cuts[part], cuts[part + 1], base, 0, unroll=2)

    bases(0)

    def returning(at, slot, head, there):
        _, _, rows, _, _ = plan[at]
        mine, _ = spot(at)
        return pltpu.make_async_remote_copy(
            src_ref=outbox[at].at[slot, there],
            dst_ref=back[at].at[head, pl.ds(0, rows)],
            send_sem=ret_send.at[seats[at] + slot],
            recv_sem=ret_recv.at[at],
            device_id=(me - mine + there,),
            device_id_type=MESH,
        )

    row16 = lax.broadcasted_iota(jnp.int32, (16, tokens), 0)
    blank = jnp.zeros((pair - size - 16, tokens), jnp.bfloat16)

    for at in order:
        _, group, rows, per, _ = plan[at]
        if at == order[-1]:
            bases(1)
        for slot in range(per):
            mine, first_owner = spot(at)
            head = first_owner * per + slot

            @pl.when(head < heads)
            def _(at=at, group=group, rows=rows, slot=slot, head=head, mine=mine):
                with jax.named_scope(f"arr{at}_{slot}"):
                    pltpu.make_async_copy(
                        inbox[at].at[slot], inbox[at].at[slot], recv_sem.at[seats[at] + slot]
                    ).wait()
                block = inbox[at][slot]
                if is_packed(rows):
                    left = block[:, :rows].reshape(tokens, pair).astype(jnp.float32)
                    right = block[:, rows:].reshape(tokens // 2, pair).astype(jnp.float32)
                    split = (group, rows // 2, pair)
                    right = jnp.concatenate(
                        [right.reshape(split), swap_halves(right).reshape(split)], 1
                    ).reshape(tokens, pair)
                else:
                    block = block.reshape(tokens, 2 * pair)
                    left = block[:, :pair].astype(jnp.float32)
                    right = block[:, pair:].astype(jnp.float32)
                value = jnp.where(low, right, 1.0).astype(jnp.bfloat16)
                query = jnp.where(low, left, 0.0).astype(jnp.bfloat16)
                key = swap_halves(left).astype(jnp.bfloat16)
                value_t = value.T[: size + 16]
                got, peak = attend(key, query, value_t)
                sums = got[size : size + 1]
                lse = peak + jnp.log(sums)
                high = lse.astype(jnp.bfloat16).astype(jnp.float32)
                rest = lse - high
                mid = rest.astype(jnp.bfloat16).astype(jnp.float32)
                parts = jnp.where(row16 == 0, high, 0.0)
                parts = jnp.where(row16 == 1, mid, parts)
                parts = jnp.where(row16 == 2, rest - mid, parts)
                result = jnp.concatenate(
                    [
                        (got[:size] / sums).astype(jnp.bfloat16),
                        parts.astype(jnp.bfloat16),
                        blank,
                    ],
                    0,
                )
                outbox[at][slot] = (
                    result.T.reshape(group, rows, pair).astype(outbox[at].dtype)
                )

                def give(step, carry):
                    returning(at, slot, head, lax.rem(mine + step, group)).start()
                    return carry

                with jax.named_scope(f"give{at}_{slot}"):
                    pltpu.make_async_copy(
                        outbox[at].at[slot, mine],
                        back[at].at[head, pl.ds(0, rows)],
                        ret_recv.at[at],
                    ).start()
                    lax.fori_loop(1, group, give, 0, unroll=group <= 32)

    bases(2)

    for at in order:
        _, group, rows, per, _ = plan[at]
        _, first_owner = spot(at)
        owned = jnp.clip(heads - first_owner * per, 0, per)
        with jax.named_scope(f"coll{at}"):
            for many in range(per + 1):

                @pl.when(owned == many)
                def _(at=at, many=many):
                    sent = stage[at].at[pl.ds(0, heads - many)]
                    pltpu.make_async_copy(sent, sent, send_sem.at[at]).wait()

            landed = back[at].at[:, pl.ds(0, rows)]
            pltpu.make_async_copy(landed, landed, ret_recv.at[at]).wait()

    for at in order:
        _, group, _, per, _ = plan[at]
        _, first_owner = spot(at)
        for slot in range(per):

            @pl.when(first_owner * per + slot < heads)
            def _(at=at, group=group, slot=slot):
                gone = outbox[at].at[slot, pl.ds(0, group - 1)]
                pltpu.make_async_copy(gone, gone, ret_send.at[seats[at] + slot]).wait()


def merge_kernel(plan, heads, base_out, base_peak, base_total, hits, *refs):
    number = len(plan)
    back = refs[:number]
    out_hbm, out_vmem, sem = refs[number:]
    tokens, model = out_vmem.shape
    size = model // heads
    pair = 2 * size
    pairs = heads // 2
    spans = [up8(entry[2]) for entry in plan]
    picked = sum(spans)
    row8 = lax.broadcasted_iota(jnp.int32, (8, picked), 0)
    col8 = lax.broadcasted_iota(jnp.int32, (8, picked), 1)
    level = jnp.zeros((8, picked), jnp.int32)
    for at in range(1, number):
        level = jnp.where(col8 >= sum(spans[:at]), at, level)
    mine = row8 == level
    flag = jnp.where(mine, 1.0, 0.0)

    def leave(p):
        cols = pl.ds(p * pair, pair)
        return pltpu.make_async_copy(out_vmem.at[:, cols], out_hbm.at[:, cols], sem.at[p])

    for p in range(pairs):
        merged = []
        for side in range(2):
            head = 2 * p + side
            blocks = []
            for at, (_, _, rows, _, _) in enumerate(plan):
                block = back[at][head].astype(jnp.float32)
                if rows % 8:
                    kept = lax.broadcasted_iota(jnp.int32, block.shape, 0) < rows
                    block = jnp.where(kept, block, 0.0)
                blocks.append(block)
            sent_t = jnp.concatenate(blocks, 0).T
            parts = [
                jnp.where(mine, sent_t[size + i : size + i + 1], 0.0) for i in range(3)
            ]
            parts = jnp.concatenate(parts + [flag], 0).astype(jnp.bfloat16)
            hit = hits[p, side * picked : (side + 1) * picked]
            lses = jnp.dot(parts, hit, preferred_element_type=jnp.float32)
            lse = lses[:8] + lses[8:16] + lses[16:24]
            lse = jnp.where(lses[24:] > 0.5, lse, base_peak[head])
            best = jnp.max(lse, axis=0, keepdims=True)
            share = jnp.exp(lse - best)
            bottom = jnp.sum(share * base_total[head], axis=0, keepdims=True)
            share = share / bottom
            spread = jnp.concatenate(
                [
                    jnp.broadcast_to(share[at : at + 1], (spans[at], tokens))
                    for at in range(number)
                ],
                0,
            )
            moved = jnp.dot(
                sent_t[:size].astype(jnp.bfloat16),
                hit * spread.astype(jnp.bfloat16),
                preferred_element_type=jnp.float32,
            )
            merged.append(moved + share[number : number + 1] * base_out[head])
        both = jnp.concatenate(merged, 0).astype(jnp.bfloat16)
        out_vmem[:, pl.ds(p * pair, pair)] = both.T
        leave(p).start()
    for p in range(pairs):
        leave(p).wait()


def exchange_body(queries, keys, values, offsets):
    tokens, model = queries.shape
    levels, heads = offsets.shape
    count = lax.axis_size("ctx")
    plan = plan_of(levels, count, tokens, heads)
    size = model // heads
    pair = 2 * size
    number = len(plan)
    seats = sum(entry[3] for entry in plan)
    picked = sum(up8(entry[2]) for entry in plan)

    def block(rows):
        return (rows + rows // 2, pair) if is_packed(rows) else (rows, 2 * pair)

    scratch = [pltpu.SMEM((levels, heads), jnp.int32)]
    scratch += [pltpu.VMEM((tokens, model), jnp.bfloat16)] * 3
    for _, group, rows, per, _ in plan:
        scratch.append(pltpu.VMEM((heads, *block(rows)), kind_of(rows)))
    for _, group, rows, per, _ in plan:
        scratch.append(pltpu.VMEM((per, group, *block(rows)), kind_of(rows)))
    for _, group, rows, per, _ in plan:
        scratch.append(pltpu.VMEM((per, group, rows, pair), kind_of(rows)))
    scratch += [
        pltpu.SemaphoreType.DMA((4,)),
        pltpu.SemaphoreType.DMA((number,)),
        pltpu.SemaphoreType.DMA((seats,)),
        pltpu.SemaphoreType.DMA((seats,)),
        pltpu.SemaphoreType.DMA((number,)),
    ]
    outs = [
        pltpu.VMEM((heads, size, tokens), jnp.float32),
        pltpu.VMEM((heads, 8, tokens), jnp.float32),
        pltpu.VMEM((heads, 8, tokens), jnp.float32),
        pltpu.VMEM((heads // 2, 2 * picked, tokens), jnp.bfloat16),
    ]
    for _, _, rows, _, _ in plan:
        outs.append(pltpu.VMEM((heads, up8(rows), pair), kind_of(rows)))
    scale = size**-0.5
    vmem = pl.BlockSpec(memory_space=pltpu.VMEM)
    far = pl.BlockSpec(memory_space=pl.ANY)
    parts = pl.pallas_call(
        functools.partial(exchange_kernel, plan, heads, scale),
        out_shape=outs,
        in_specs=[far, far, far, far],
        out_specs=[vmem] * len(outs),
        scratch_shapes=scratch,
        compiler_params=pltpu.CompilerParams(collective_id=0, has_side_effects=True),
    )(offsets, queries, keys, values)
    return pl.pallas_call(
        functools.partial(merge_kernel, plan, heads),
        out_shape=jax.ShapeDtypeStruct((tokens, model), jnp.bfloat16),
        in_specs=[vmem] * len(outs),
        out_specs=far,
        scratch_shapes=[
            pltpu.VMEM((tokens, model), jnp.bfloat16),
            pltpu.SemaphoreType.DMA((heads // 2,)),
        ],
        compiler_params=pltpu.CompilerParams(vmem_limit_bytes=16 * 1024 * 1024),
    )(*parts)


def solution(mesh):
    in_specs = (P("ctx", None), P("ctx", None), P("ctx", None), P())
    out_specs = P("ctx", None)
    return jax.shard_map(
        exchange_body, mesh=mesh, in_specs=in_specs, out_specs=out_specs, check_vma=False
    )
```

time: 27.2 us -> 19.8 us (0.73)
  the two profiles are of different devices: /device:TPU:17 before, /device:TPU:0 now
where the time goes in v1:
time: 19.8 us; the launch traced here: 19.6 us
  Pallas kernels  19.6 us (99%)
    pallas_call x1, Pallas kernels, exchange_body(): pl.pallas_call(functools.partial(exchange_kernel, plan, heads, scale), ou...  17.5 us
    pallas_call x1, Pallas kernels, exchange_body(): pl.pallas_call(functools.partial(merge_kernel, plan, heads), out_shape=ja...  2.09 us

profile of v1, /device:TPU:0, one launch (start us, length us, event | category | flops | bytes accessed | tf_op | source)
XLA Modules:
  0.0 19.6 jit_solution(7299270767246280952)
XLA Ops:
  0.0 17.5 %shard_map.46 = (f32[12,64,256]{2,1,0:T(8,128)S(1)}, f32[12,8,256]{2,1,0:T(8,128)S(1)}, f32[12,8,256]{2,1,0:T(8,128)S(1)}, bf16[6,192,256]{2,1,0:T(8,128)(2,1)S(...) custom-call(s32[5,12]{1,0:T(8,128)} %offs_hbm.1, ...), custom_call_target="tpu_custom_call" | custom-call | tf_op jit(solution)/shard_map/pallas_call | solution.py:452
  17.5 2.1 %shard_map.47 = bf16[256,768]{1,0:T(8,128)(2,1)} custom-call(f32[12,64,256]{2,1,0:T(8,128)S(1)} %get-tuple-element.13.base_out, f32[12,8,256]{2,1,0:T(8,128)S(1)} %get-tuple-element.14.base_peak, f32[12,8,256]{2,1,0:T(8,128)S(1)} %get-tuple-element.15.base_total, bf16[6,192,256]{2,1,0:T(8,128)(2,1)S(1)} %get-tuple-element.16.hits, ...), custom_call_target="tpu_custom_call" | custom-call | tf_op jit(solution)/shard_map/pallas_call | solution.py:460

commit v2 on v1

--- a/solution.py
+++ b/solution.py
@@ -20,14 +20,26 @@
         per = -(-heads // group)
         shift = 0
         if group >= 2 * heads:
-            shift = group // 4 + (group // 2 - heads if late else 0)
+            shift = (group // 4 + (1 if late else -1) * (group // 2 - heads)) % group
             late = not late
         plan.append((height, group, tokens // group, per, shift))
     return plan
 
 
 def is_packed(rows):
+    return rows % 16 == 0
+
+
+def is_folded(rows):
     return rows % 32 == 0
+
+
+def returned(rows):
+    return rows // 2 + 8 if is_folded(rows) else rows
+
+
+def held(rows):
+    return rows // 2 + 8 if is_folded(rows) else up8(rows)
 
 
 def up8(rows):
@@ -183,30 +195,30 @@
         return mine, lax.rem(mine + group - shift, group)
 
     order = list(range(number))[::-1]
-    with jax.named_scope("push"):
-        for at in order:
-            _, group, _, per, shift = plan[at]
-            mine, _ = spot(at)
-            for head in sorted(range(heads), key=lambda h: h % per):
-                where = (shift + head // per) % group
-                slot = head % per
-                target = inbox[at].at[slot, mine]
-                arrived = recv_sem.at[seats[at] + slot]
-
-                @pl.when(mine != where)
-                def _(at=at, head=head, where=where, target=target, arrived=arrived, mine=mine):
-                    pltpu.make_async_remote_copy(
-                        src_ref=stage[at].at[head],
-                        dst_ref=target,
-                        send_sem=send_sem.at[at],
-                        recv_sem=arrived,
-                        device_id=(me - mine + where,),
-                        device_id_type=MESH,
-                    ).start()
-
-                @pl.when(mine == where)
-                def _(at=at, head=head, target=target, arrived=arrived):
-                    pltpu.make_async_copy(stage[at].at[head], target, arrived).start()
+
+    def push(at):
+        _, group, _, per, shift = plan[at]
+        mine, _ = spot(at)
+        for head in sorted(range(heads), key=lambda h: h % per):
+            where = (shift + head // per) % group
+            slot = head % per
+            target = inbox[at].at[slot, mine]
+            arrived = recv_sem.at[seats[at] + slot]
+
+            @pl.when(mine != where)
+            def _(head=head, where=where, target=target, arrived=arrived):
+                pltpu.make_async_remote_copy(
+                    src_ref=stage[at].at[head],
+                    dst_ref=target,
+                    send_sem=send_sem.at[at],
+                    recv_sem=arrived,
+                    device_id=(me - mine + where,),
+                    device_id_type=MESH,
+                ).start()
+
+            @pl.when(mine == where)
+            def _(head=head, target=target, arrived=arrived):
+                pltpu.make_async_copy(stage[at].at[head], target, arrived).start()
 
     ones = jnp.ones((16, tokens), jnp.bfloat16)
     row8 = lax.broadcasted_iota(jnp.int32, (8, tokens), 0)
@@ -229,13 +241,11 @@
             base_total[head] = jnp.where(row8 == number, got[size : size + 1], 1.0)
         return carry
 
-    cuts = [pairs * part // 3 for part in range(4)]
-
-    def bases(part):
-        with jax.named_scope(f"base{part}"):
-            lax.fori_loop(cuts[part], cuts[part + 1], base, 0, unroll=2)
-
-    bases(0)
+    def bases(start, stop):
+        start, stop = pairs * start // 6, pairs * stop // 6
+        with jax.named_scope(f"base{start}"):
+            lax.fori_loop(start, stop, base, 0, unroll=2)
+
 
     def returning(at, slot, head, there):
         _, _, rows, _, _ = plan[at]
@@ -252,71 +262,79 @@
     row16 = lax.broadcasted_iota(jnp.int32, (16, tokens), 0)
     blank = jnp.zeros((pair - size - 16, tokens), jnp.bfloat16)
 
-    for at in order:
+    def serve(at, slot):
         _, group, rows, per, _ = plan[at]
-        if at == order[-1]:
-            bases(1)
-        for slot in range(per):
-            mine, first_owner = spot(at)
-            head = first_owner * per + slot
-
-            @pl.when(head < heads)
-            def _(at=at, group=group, rows=rows, slot=slot, head=head, mine=mine):
-                with jax.named_scope(f"arr{at}_{slot}"):
-                    pltpu.make_async_copy(
-                        inbox[at].at[slot], inbox[at].at[slot], recv_sem.at[seats[at] + slot]
-                    ).wait()
-                block = inbox[at][slot]
-                if is_packed(rows):
-                    left = block[:, :rows].reshape(tokens, pair).astype(jnp.float32)
-                    right = block[:, rows:].reshape(tokens // 2, pair).astype(jnp.float32)
-                    split = (group, rows // 2, pair)
-                    right = jnp.concatenate(
-                        [right.reshape(split), swap_halves(right).reshape(split)], 1
-                    ).reshape(tokens, pair)
-                else:
-                    block = block.reshape(tokens, 2 * pair)
-                    left = block[:, :pair].astype(jnp.float32)
-                    right = block[:, pair:].astype(jnp.float32)
-                value = jnp.where(low, right, 1.0).astype(jnp.bfloat16)
-                query = jnp.where(low, left, 0.0).astype(jnp.bfloat16)
-                key = swap_halves(left).astype(jnp.bfloat16)
-                value_t = value.T[: size + 16]
-                got, peak = attend(key, query, value_t)
-                sums = got[size : size + 1]
-                lse = peak + jnp.log(sums)
-                high = lse.astype(jnp.bfloat16).astype(jnp.float32)
-                rest = lse - high
-                mid = rest.astype(jnp.bfloat16).astype(jnp.float32)
-                parts = jnp.where(row16 == 0, high, 0.0)
-                parts = jnp.where(row16 == 1, mid, parts)
-                parts = jnp.where(row16 == 2, rest - mid, parts)
-                result = jnp.concatenate(
-                    [
-                        (got[:size] / sums).astype(jnp.bfloat16),
-                        parts.astype(jnp.bfloat16),
-                        blank,
-                    ],
-                    0,
-                )
-                outbox[at][slot] = (
-                    result.T.reshape(group, rows, pair).astype(outbox[at].dtype)
-                )
-
-                def give(step, carry):
-                    returning(at, slot, head, lax.rem(mine + step, group)).start()
-                    return carry
-
-                with jax.named_scope(f"give{at}_{slot}"):
-                    pltpu.make_async_copy(
-                        outbox[at].at[slot, mine],
-                        back[at].at[head, pl.ds(0, rows)],
-                        ret_recv.at[at],
-                    ).start()
-                    lax.fori_loop(1, group, give, 0, unroll=group <= 32)
-
-    bases(2)
-
+        mine, first_owner = spot(at)
+        head = first_owner * per + slot
+
+        @pl.when(head < heads)
+        def _():
+            with jax.named_scope(f"arr{at}_{slot}"):
+                pltpu.make_async_copy(
+                    inbox[at].at[slot], inbox[at].at[slot], recv_sem.at[seats[at] + slot]
+                ).wait()
+            block = inbox[at][slot]
+            if is_packed(rows):
+                left = block[:, :rows].reshape(tokens, pair).astype(jnp.float32)
+                right = block[:, rows:].reshape(tokens // 2, pair).astype(jnp.float32)
+                split = (group, rows // 2, pair)
+                right = jnp.concatenate(
+                    [right.reshape(split), swap_halves(right).reshape(split)], 1
+                ).reshape(tokens, pair)
+            else:
+                block = block.reshape(tokens, 2 * pair)
+                left = block[:, :pair].astype(jnp.float32)
+                right = block[:, pair:].astype(jnp.float32)
+            value = jnp.where(low, right, 1.0).astype(jnp.bfloat16)
+            query = jnp.where(low, left, 0.0).astype(jnp.bfloat16)
+            key = swap_halves(left).astype(jnp.bfloat16)
+            value_t = value.T[: size + 16]
+            got, peak = attend(key, query, value_t)
+            sums = got[size : size + 1]
+            lse = peak + jnp.log(sums)
+            high = lse.astype(jnp.bfloat16).astype(jnp.float32)
+            rest = lse - high
+            mid = rest.astype(jnp.bfloat16).astype(jnp.float32)
+            parts = jnp.where(row16 == 0, high, 0.0)
+            parts = jnp.where(row16 == 1, mid, parts)
+            parts = jnp.where(row16 == 2, rest - mid, parts)
+            result = jnp.concatenate(
+                [
+                    (got[:size] / sums).astype(jnp.bfloat16),
+                    parts.astype(jnp.bfloat16),
+                    blank,
+                ],
+                0,
+            )
+            outbox[at][slot] = (
+                result.T.reshape(group, rows, pair).astype(outbox[at].dtype)
+            )
+
+            def give(step, carry):
+                returning(at, slot, head, lax.rem(mine + step, group)).start()
+                return carry
+
+            with jax.named_scope(f"give{at}_{slot}"):
+                pltpu.make_async_copy(
+                    outbox[at].at[slot, mine],
+                    back[at].at[head, pl.ds(0, rows)],
+                    ret_recv.at[at],
+                ).start()
+                lax.fori_loop(1, group, give, 0, unroll=group <= 32)
+
+    for at in order[:-1]:
+        with jax.named_scope(f"push{at}"):
+            push(at)
+    bases(0, 2)
+    with jax.named_scope("push0"):
+        push(0)
+    bases(2, 4)
+    for at in order[:-1]:
+        for slot in range(plan[at][3]):
+            serve(at, slot)
+    for slot in range(plan[0][3]):
+        serve(0, slot)
+    bases(4, 6)
     for at in order:
         _, group, rows, per, _ = plan[at]
         _, first_owner = spot(at)
@@ -365,8 +383,8 @@
         cols = pl.ds(p * pair, pair)
         return pltpu.make_async_copy(out_vmem.at[:, cols], out_hbm.at[:, cols], sem.at[p])
 
+    sents, sums, shares = {}, {}, {}
     for p in range(pairs):
-        merged = []
         for side in range(2):
             head = 2 * p + side
             blocks = []
@@ -376,19 +394,30 @@
                     kept = lax.broadcasted_iota(jnp.int32, block.shape, 0) < rows
                     block = jnp.where(kept, block, 0.0)
                 blocks.append(block)
-            sent_t = jnp.concatenate(blocks, 0).T
-            parts = [
-                jnp.where(mine, sent_t[size + i : size + i + 1], 0.0) for i in range(3)
-            ]
+            sent_t = jnp.concatenate(blocks, 0).astype(jnp.bfloat16).T
+            hit = hits[p, side * picked : (side + 1) * picked]
+            tails = sent_t[size : size + 16].astype(jnp.float32)
+            parts = [jnp.where(mine, tails[i : i + 1], 0.0) for i in range(3)]
             parts = jnp.concatenate(parts + [flag], 0).astype(jnp.bfloat16)
-            hit = hits[p, side * picked : (side + 1) * picked]
             lses = jnp.dot(parts, hit, preferred_element_type=jnp.float32)
+            sents[head], sums[head] = sent_t, lses
+    for p in range(pairs):
+        for side in range(2):
+            head = 2 * p + side
+            lses = sums[head]
             lse = lses[:8] + lses[8:16] + lses[16:24]
             lse = jnp.where(lses[24:] > 0.5, lse, base_peak[head])
             best = jnp.max(lse, axis=0, keepdims=True)
             share = jnp.exp(lse - best)
             bottom = jnp.sum(share * base_total[head], axis=0, keepdims=True)
             share = share / bottom
+            shares[head] = share
+    for p in range(pairs):
+        merged = []
+        for side in range(2):
+            head = 2 * p + side
+            sent_t, share = sents[head], shares[head]
+            hit = hits[p, side * picked : (side + 1) * picked]
             spread = jnp.concatenate(
                 [
                     jnp.broadcast_to(share[at : at + 1], (spans[at], tokens))
@@ -397,7 +426,7 @@
                 0,
             )
             moved = jnp.dot(
-                sent_t[:size].astype(jnp.bfloat16),
+                sent_t[:size],
                 hit * spread.astype(jnp.bfloat16),
                 preferred_element_type=jnp.float32,
             )

time: 19.8 us -> 18.7 us (0.944)
  Pallas kernels: 19.6 us -> 18.6 us
    pallas_call x1, Pallas kernels: 2.09 us -> 1.3 us  [exchange_body(): pl.pallas_call(functools.partial(merge_kernel, plan, heads), out_shape=ja...]
    pallas_call x1, Pallas kernels: 17.5 us -> 17.3 us  [exchange_body(): pl.pallas_call(functools.partial(exchange_kernel, plan, heads, scale), ou...]
where the time goes in v2:
time: 18.7 us; the launch traced here: 18.6 us
  Pallas kernels  18.6 us (99%)
    pallas_call x1, Pallas kernels, exchange_body(): pl.pallas_call(functools.partial(exchange_kernel, plan, heads, scale), ou...  17.3 us
    pallas_call x1, Pallas kernels, exchange_body(): pl.pallas_call(functools.partial(merge_kernel, plan, heads), out_shape=ja...  1.3 us

profile of v2, /device:TPU:0, one launch (start us, length us, event | category | flops | bytes accessed | tf_op | source)
XLA Modules:
  0.0 18.6 jit_solution(15724889437483272051)
XLA Ops:
  0.0 17.3 %shard_map.46 = (f32[12,64,256]{2,1,0:T(8,128)S(1)}, f32[12,8,256]{2,1,0:T(8,128)S(1)}, f32[12,8,256]{2,1,0:T(8,128)S(1)}, bf16[6,192,256]{2,1,0:T(8,128)(2,1)S(...) custom-call(s32[5,12]{1,0:T(8,128)} %offs_hbm.1, ...), custom_call_target="tpu_custom_call" | custom-call | tf_op jit(solution)/shard_map/pallas_call | solution.py:481
  17.3 1.3 %shard_map.47 = bf16[256,768]{1,0:T(8,128)(2,1)} custom-call(f32[12,64,256]{2,1,0:T(8,128)S(1)} %get-tuple-element.13.base_out, f32[12,8,256]{2,1,0:T(8,128)S(1)} %get-tuple-element.14.base_peak, f32[12,8,256]{2,1,0:T(8,128)S(1)} %get-tuple-element.15.base_total, bf16[6,192,256]{2,1,0:T(8,128)(2,1)S(1)} %get-tuple-element.16.hits, ...), custom_call_target="tpu_custom_call" | custom-call | tf_op jit(solution)/shard_map/pallas_call | solution.py:489

commit v3 on v2

--- a/solution.py
+++ b/solution.py
@@ -9,37 +9,29 @@
 
 MESH = pl.DeviceIdType.MESH
 NEG = -1e30
+LINE = 4
 LAST = (((1,), (1,)), ((), ()))
 
 
 def plan_of(levels, count, tokens, heads):
     plan = []
-    late = False
+    wide = 0
     for height in range(1, levels):
         group = min(4**height, count)
         per = -(-heads // group)
-        shift = 0
+        first, step = 0, 1
         if group >= 2 * heads:
-            shift = (group // 4 + (1 if late else -1) * (group // 2 - heads)) % group
-            late = not late
-        plan.append((height, group, tokens // group, per, shift))
+            first, step = wide % 2, 2
+            wide += 1
+        elif group > heads:
+            first = group - heads
+        owners = [first + step * (head // per) for head in range(heads)]
+        plan.append((height, group, tokens // group, per, owners))
     return plan
 
 
 def is_packed(rows):
     return rows % 16 == 0
-
-
-def is_folded(rows):
-    return rows % 32 == 0
-
-
-def returned(rows):
-    return rows // 2 + 8 if is_folded(rows) else rows
-
-
-def held(rows):
-    return rows // 2 + 8 if is_folded(rows) else up8(rows)
 
 
 def up8(rows):
@@ -105,7 +97,7 @@
     stage = refs[:number]
     inbox = refs[number : 2 * number]
     outbox = refs[2 * number : 3 * number]
-    in_sem, send_sem, recv_sem, ret_send, ret_recv = refs[3 * number :]
+    in_sem, send_sem, recv_sem, ret_send, ret_recv, high_sem = refs[3 * number :]
     tokens, model = q_ref.shape
     size = model // heads
     pair = 2 * size
@@ -122,14 +114,32 @@
         load.start()
 
     barrier = pltpu.get_barrier_semaphore()
+    block = count // LINE
+    line = lax.div(me, block)
+    seat_in = me - line * block
+
+    def tell(sem, other):
+        pl.semaphore_signal(sem, inc=1, device_id=(other,), device_id_type=MESH)
 
     def greet(step, carry):
-        other = lax.rem(me + step, count)
-        pl.semaphore_signal(barrier, inc=1, device_id=(other,), device_id_type=MESH)
+        tell(barrier, line * block + lax.rem(seat_in + step, block))
         return carry
 
+    def greet_above(step, carry):
+        tell(barrier, line * block + block + step)
+        return carry
+
     with jax.named_scope("greet"):
-        lax.fori_loop(1, count, greet, 0)
+        lax.fori_loop(1, block, greet, 0)
+        lax.fori_loop(0, (LINE - 1 - line) * block, greet_above, 0)
+
+    def hear(first, last):
+        for at in range(LINE):
+            for above in range(max(first, at + 1), last + 1):
+
+                @pl.when(line == at)
+                def _(above=above):
+                    pl.semaphore_wait(high_sem.at[above], 1)
 
     low = halves((tokens, pair))
     spans = [up8(entry[2]) for entry in plan]
@@ -137,6 +147,23 @@
     picked = sum(spans)
     low_p = halves((picked, pair))
     where_p = places(plan, tokens)
+
+    def meet():
+        with jax.named_scope("barw"):
+            pl.semaphore_wait(barrier, block - 1 + line * block)
+
+        for at in range(1, LINE):
+            for below in range(at):
+
+                @pl.when(line == at)
+                def _(at=at, below=below):
+                    tell(high_sem.at[at], me - (at - below) * block)
+
+    soon = line < LINE // 2
+
+    @pl.when(jnp.logical_not(soon))
+    def _():
+        meet()
 
     with jax.named_scope("loadw"):
         for load in loads:
@@ -163,7 +190,7 @@
                 query = swap_halves(query)
                 value, swapped = swapped, value
             left = jnp.where(low_p, query * scale, key)
-            for at, (_, _, rows, _, _) in enumerate(plan):
+            for at, (_, _, rows, *_) in enumerate(plan):
                 kind = stage[at].dtype
                 first = starts[at]
                 last = first + rows
@@ -181,27 +208,36 @@
 
     with jax.named_scope("pick"):
         lax.fori_loop(0, pairs, pick, 0, unroll=3)
-    with jax.named_scope("barw"):
-        pl.semaphore_wait(barrier, count - 1)
+    @pl.when(soon)
+    def _():
+        meet()
 
     seats, seat = [], 0
-    for _, _, _, per, _ in plan:
+    for _, _, _, per, *_ in plan:
         seats.append(seat)
         seat += per
 
     def spot(at):
-        _, group, _, _, shift = plan[at]
+        _, group, _, per, owners = plan[at]
         mine = lax.rem(me, group)
-        return mine, lax.rem(mine + group - shift, group)
-
+        found = heads
+        for head in range(0, heads, per):
+            found = jnp.where(mine == owners[head], head, found)
+        return mine, found
+
+    spots = [spot(at) for at in range(number)]
     order = list(range(number))[::-1]
 
-    def push(at):
-        _, group, _, per, shift = plan[at]
-        mine, _ = spot(at)
+    def push(at, slots=None, only=None):
+        _, group, _, per, *_ = plan[at]
+        mine, _ = spots[at]
         for head in sorted(range(heads), key=lambda h: h % per):
-            where = (shift + head // per) % group
+            where = plan[at][4][head]
             slot = head % per
+            if only is not None and head != only:
+                continue
+            if slots is not None and slot not in slots:
+                continue
             target = inbox[at].at[slot, mine]
             arrived = recv_sem.at[seats[at] + slot]
 
@@ -248,8 +284,8 @@
 
 
     def returning(at, slot, head, there):
-        _, _, rows, _, _ = plan[at]
-        mine, _ = spot(at)
+        _, _, rows, *_ = plan[at]
+        mine, _ = spots[at]
         return pltpu.make_async_remote_copy(
             src_ref=outbox[at].at[slot, there],
             dst_ref=back[at].at[head, pl.ds(0, rows)],
@@ -263,9 +299,9 @@
     blank = jnp.zeros((pair - size - 16, tokens), jnp.bfloat16)
 
     def serve(at, slot):
-        _, group, rows, per, _ = plan[at]
-        mine, first_owner = spot(at)
-        head = first_owner * per + slot
+        _, group, rows, per, *_ = plan[at]
+        mine, first = spots[at]
+        head = first + slot
 
         @pl.when(head < heads)
         def _():
@@ -322,23 +358,82 @@
                 ).start()
                 lax.fori_loop(1, group, give, 0, unroll=group <= 32)
 
-    for at in order[:-1]:
-        with jax.named_scope(f"push{at}"):
+    last = line == LINE - 1
+    soon_slots = range(1)
+    rest_slots = range(1, plan[0][3])
+
+    @pl.when(jnp.logical_not(last))
+    def _():
+        with jax.named_scope("push0"):
+            push(0, soon_slots)
+
+    @pl.when(soon)
+    def _():
+        bases(0, 2)
+
+    far = [at for at in order if plan[at][1] >= 2 * heads]
+    close = [at for at in order[:-1] if at not in far]
+
+    @pl.when(soon)
+    def _():
+        hear(1, 1)
+        for at in close:
             push(at)
-    bases(0, 2)
-    with jax.named_scope("push0"):
-        push(0)
-    bases(2, 4)
-    for at in order[:-1]:
-        for slot in range(plan[at][3]):
+
+    with jax.named_scope("hear"):
+        hear(2, LINE - 2)
+    with jax.named_scope("push1"):
+        for head in range(heads):
+            for at in far:
+                push(at, only=head)
+
+    @pl.when(jnp.logical_not(soon))
+    def _():
+        hear(LINE - 1, LINE - 1)
+        for at in close:
+            push(at)
+
+    @pl.when(last)
+    def _():
+        with jax.named_scope("push0b"):
+            push(0)
+
+    @pl.when(jnp.logical_not(last))
+    def _():
+        with jax.named_scope("push0c"):
+            push(0, rest_slots)
+
+    with jax.named_scope("late"):
+        pl.when(soon)(lambda: hear(LINE - 1, LINE - 1))
+
+    @pl.when(jnp.logical_not(soon))
+    def _():
+        bases(0, 2)
+
+    wide = [(at, slot) for at in order[:-1] for slot in range(plan[at][3])]
+    tall = [(0, slot) for slot in range(plan[0][3])]
+
+    def serve_all(jobs):
+        for at, slot in jobs:
             serve(at, slot)
-    for slot in range(plan[0][3]):
-        serve(0, slot)
-    bases(4, 6)
+
+    @pl.when(last)
+    def _():
+        serve_all(wide + tall)
+
+    @pl.when(soon)
+    def _():
+        serve_all(tall[:1] + wide[-1:] + wide[:-1] + tall[1:])
+
+    @pl.when(jnp.logical_not(jnp.logical_or(soon, last)))
+    def _():
+        serve_all(tall[:1] + wide + tall[1:])
+
+    bases(2, 6)
     for at in order:
-        _, group, rows, per, _ = plan[at]
-        _, first_owner = spot(at)
-        owned = jnp.clip(heads - first_owner * per, 0, per)
+        _, group, rows, per, *_ = plan[at]
+        _, first = spots[at]
+        owned = jnp.clip(heads - first, 0, per)
         with jax.named_scope(f"coll{at}"):
             for many in range(per + 1):
 
@@ -351,11 +446,11 @@
             pltpu.make_async_copy(landed, landed, ret_recv.at[at]).wait()
 
     for at in order:
-        _, group, _, per, _ = plan[at]
-        _, first_owner = spot(at)
+        _, group, _, per, *_ = plan[at]
+        _, first = spots[at]
         for slot in range(per):
 
-            @pl.when(first_owner * per + slot < heads)
+            @pl.when(first + slot < heads)
             def _(at=at, group=group, slot=slot):
                 gone = outbox[at].at[slot, pl.ds(0, group - 1)]
                 pltpu.make_async_copy(gone, gone, ret_send.at[seats[at] + slot]).wait()
@@ -388,7 +483,7 @@
         for side in range(2):
             head = 2 * p + side
             blocks = []
-            for at, (_, _, rows, _, _) in enumerate(plan):
+            for at, (_, _, rows, *_) in enumerate(plan):
                 block = back[at][head].astype(jnp.float32)
                 if rows % 8:
                     kept = lax.broadcasted_iota(jnp.int32, block.shape, 0) < rows
@@ -454,11 +549,11 @@
 
     scratch = [pltpu.SMEM((levels, heads), jnp.int32)]
     scratch += [pltpu.VMEM((tokens, model), jnp.bfloat16)] * 3
-    for _, group, rows, per, _ in plan:
+    for _, group, rows, per, *_ in plan:
         scratch.append(pltpu.VMEM((heads, *block(rows)), kind_of(rows)))
-    for _, group, rows, per, _ in plan:
+    for _, group, rows, per, *_ in plan:
         scratch.append(pltpu.VMEM((per, group, *block(rows)), kind_of(rows)))
-    for _, group, rows, per, _ in plan:
+    for _, group, rows, per, *_ in plan:
         scratch.append(pltpu.VMEM((per, group, rows, pair), kind_of(rows)))
     scratch += [
         pltpu.SemaphoreType.DMA((4,)),
@@ -466,6 +561,7 @@
         pltpu.SemaphoreType.DMA((seats,)),
         pltpu.SemaphoreType.DMA((seats,)),
         pltpu.SemaphoreType.DMA((number,)),
+        pltpu.SemaphoreType.REGULAR((LINE,)),
     ]
     outs = [
         pltpu.VMEM((heads, size, tokens), jnp.float32),
@@ -473,7 +569,7 @@
         pltpu.VMEM((heads, 8, tokens), jnp.float32),
         pltpu.VMEM((heads // 2, 2 * picked, tokens), jnp.bfloat16),
     ]
-    for _, _, rows, _, _ in plan:
+    for _, _, rows, *_ in plan:
         outs.append(pltpu.VMEM((heads, up8(rows), pair), kind_of(rows)))
     scale = size**-0.5
     vmem = pl.BlockSpec(memory_space=pltpu.VMEM)

time: 18.7 us -> 17.9 us (0.957)
  Pallas kernels: 18.6 us -> 17.7 us
    pallas_call x1, Pallas kernels: 17.3 us -> 16.4 us  [exchange_body(): pl.pallas_call(functools.partial(exchange_kernel, plan, heads, scale), ou...]
where the time goes in v3:
time: 17.9 us; the launch traced here: 17.7 us
  Pallas kernels  17.7 us (99%)
    pallas_call x1, Pallas kernels, exchange_body(): pl.pallas_call(functools.partial(exchange_kernel, plan, heads, scale), ou...  16.4 us
    pallas_call x1, Pallas kernels, exchange_body(): pl.pallas_call(functools.partial(merge_kernel, plan, heads), out_shape=ja...  1.3 us

profile of v3, /device:TPU:0, one launch (start us, length us, event | category | flops | bytes accessed | tf_op | source)
XLA Modules:
  0.0 17.7 jit_solution(17116095891097726023)
XLA Ops:
  0.0 16.4 %shard_map.46 = (f32[12,64,256]{2,1,0:T(8,128)S(1)}, f32[12,8,256]{2,1,0:T(8,128)S(1)}, f32[12,8,256]{2,1,0:T(8,128)S(1)}, bf16[6,192,256]{2,1,0:T(8,128)(2,1)S(...) custom-call(s32[5,12]{1,0:T(8,128)} %offs_hbm.1, ...), custom_call_target="tpu_custom_call" | custom-call | tf_op jit(solution)/shard_map/pallas_call | solution.py:577
  16.4 1.3 %shard_map.47 = bf16[256,768]{1,0:T(8,128)(2,1)} custom-call(f32[12,64,256]{2,1,0:T(8,128)S(1)} %get-tuple-element.13.base_out, f32[12,8,256]{2,1,0:T(8,128)S(1)} %get-tuple-element.14.base_peak, f32[12,8,256]{2,1,0:T(8,128)S(1)} %get-tuple-element.15.base_total, bf16[6,192,256]{2,1,0:T(8,128)(2,1)S(1)} %get-tuple-element.16.hits, ...), custom_call_target="tpu_custom_call" | custom-call | tf_op jit(solution)/shard_map/pallas_call | solution.py:585

commit v4 on v3

--- a/solution.py
+++ b/solution.py
@@ -207,7 +207,7 @@
         return carry
 
     with jax.named_scope("pick"):
-        lax.fori_loop(0, pairs, pick, 0, unroll=3)
+        lax.fori_loop(0, pairs, pick, 0, unroll=6)
     @pl.when(soon)
     def _():
         meet()
@@ -346,8 +346,11 @@
                 result.T.reshape(group, rows, pair).astype(outbox[at].dtype)
             )
 
-            def give(step, carry):
-                returning(at, slot, head, lax.rem(mine + step, group)).start()
+            def give(there, carry):
+                @pl.when(there != mine)
+                def _():
+                    returning(at, slot, head, there).start()
+
                 return carry
 
             with jax.named_scope(f"give{at}_{slot}"):
@@ -356,7 +359,7 @@
                     back[at].at[head, pl.ds(0, rows)],
                     ret_recv.at[at],
                 ).start()
-                lax.fori_loop(1, group, give, 0, unroll=group <= 32)
+                lax.fori_loop(0, group, give, 0, unroll=group <= 32)
 
     last = line == LINE - 1
     soon_slots = range(1)

time: 17.9 us -> 17.6 us (0.983)
  Pallas kernels: 17.7 us -> 17.4 us
    pallas_call x1, Pallas kernels: 16.4 us -> 16.1 us  [exchange_body(): pl.pallas_call(functools.partial(exchange_kernel, plan, heads, scale), ou...]
where the time goes in v4:
time: 17.6 us; the launch traced here: 17.5 us
  Pallas kernels  17.4 us (99%)
    pallas_call x1, Pallas kernels, exchange_body(): pl.pallas_call(functools.partial(exchange_kernel, plan, heads, scale), ou...  16.1 us
    pallas_call x1, Pallas kernels, exchange_body(): pl.pallas_call(functools.partial(merge_kernel, plan, heads), out_shape=ja...  1.3 us

profile of v4, /device:TPU:0, one launch (start us, length us, event | category | flops | bytes accessed | tf_op | source)
XLA Modules:
  0.0 17.5 jit_solution(13447506257986160950)
XLA Ops:
  0.0 16.1 %shard_map.46 = (f32[12,64,256]{2,1,0:T(8,128)S(1)}, f32[12,8,256]{2,1,0:T(8,128)S(1)}, f32[12,8,256]{2,1,0:T(8,128)S(1)}, bf16[6,192,256]{2,1,0:T(8,128)(2,1)S(...) custom-call(s32[5,12]{1,0:T(8,128)} %offs_hbm.1, ...), custom_call_target="tpu_custom_call" | custom-call | tf_op jit(solution)/shard_map/pallas_call | solution.py:580
  16.2 1.3 %shard_map.47 = bf16[256,768]{1,0:T(8,128)(2,1)} custom-call(f32[12,64,256]{2,1,0:T(8,128)S(1)} %get-tuple-element.13.base_out, f32[12,8,256]{2,1,0:T(8,128)S(1)} %get-tuple-element.14.base_peak, f32[12,8,256]{2,1,0:T(8,128)S(1)} %get-tuple-element.15.base_total, bf16[6,192,256]{2,1,0:T(8,128)(2,1)S(1)} %get-tuple-element.16.hits, ...), custom_call_target="tpu_custom_call" | custom-call | tf_op jit(solution)/shard_map/pallas_call | solution.py:588
